TPU v7x, 128 devices: a whole 4x4x4 slice. The times are simulated.
128 devices in a mesh: task: 8 (over x, core), param: 16 (over y, z).
Axes of the slice: x: 4, y: 4, z: 4, core: 2. Of those that a mesh axis runs over, the one named last changes fastest.
Arguments:
- acts: bfloat16 [128, 3584], replicated, may hold values from -6 to 6
- out_grads: bfloat16 [8, 128, 10240], P('task', None, 'param'), may hold values from -12 to 12
- order: int32 [8], replicated, may hold values from 0 to 7, each once
Outputs:
- update: float32 [3584, 10240], P('task', 'param')
- weights: float32 [8], replicated
All inputs are finite; a program needn't handle non-finite values.
Results may differ from a plain program's by a relative error of at most 0.0029.
Values may be sent and summed in bfloat16 or wider, within the bound.
No kernel may reach another device: no remote copies, remote signals or barrier semaphores. Data moves between devices by JAX's collectives and lax.ppermute only.
A program may use at most 64 MiB of HBM per device.

v0:
```python
import jax
import jax.numpy as jnp
from jax import lax
from jax.experimental import pallas as pl
from jax.experimental.pallas import tpu as pltpu
from jax.sharding import Mesh
from jax.sharding import PartitionSpec as P

TASK = ("task_0", "task_1")
PARAM = ("param_0", "param_1")
LANES = 128
ORDER = (3, 1, 2)
FLIP = (2,)
VMEM = pl.BlockSpec(memory_space=pltpu.VMEM)


def params(mib):
    return pltpu.CompilerParams(vmem_limit_bytes=mib << 20)


def chip_at(offset):
    return lax.bitwise_xor(lax.axis_index("task_0"), offset)


def prepare_kernel(
    order_hbm, acts_hbm, own_hbm, outer_ref, rows_ref, turns_ref, own_ref,
    order_ref, acts_ref, both_ref, sems,
):
    copies = [
        pltpu.make_async_copy(acts_hbm, acts_ref, sems.at[0]),
        pltpu.make_async_copy(order_hbm, order_ref, sems.at[1]),
        pltpu.make_async_copy(own_hbm, own_ref, sems.at[2]),
    ]
    for copy in copies:
        copy.start()
    task = lax.axis_index("task_0") * 2 + lax.axis_index("task_1")
    tasks = turns_ref.shape[0]
    span = both_ref.shape[0]
    count = rows_ref.shape[0]
    base = (task // 2) * span
    copies[0].wait()
    outer_ref[...] = lax.dot_general(
        acts_ref[...], acts_ref[...], (((1,), (1,)), ((), ())), preferred_element_type=jnp.float32
    )
    for at in range(0, span, LANES):
        part = acts_ref[:, pl.ds(pl.multiple_of(base + at, LANES), LANES)]
        both_ref[at : at + LANES] = part.T
    rows_ref[...] = both_ref[pl.ds(pl.multiple_of((task % 2) * count, 64), count)]
    copies[1].wait()
    for step in range(tasks):
        turns_ref[step] = jnp.full((tasks, LANES), order_ref[step], jnp.int32)
    copies[2].wait()


def prepare(order, acts, own):
    tokens, depth = acts.shape
    tasks = order.shape[0]
    rows = depth // tasks
    return pl.pallas_call(
        prepare_kernel,
        out_shape=(
            jax.ShapeDtypeStruct((tokens, tokens), jnp.float32),
            jax.ShapeDtypeStruct((rows, tokens), acts.dtype),
            jax.ShapeDtypeStruct((tasks, tasks, LANES), jnp.int32),
            jax.ShapeDtypeStruct(own.shape, own.dtype),
        ),
        in_specs=[pl.BlockSpec(memory_space=pltpu.HBM)] * 3,
        out_specs=(VMEM,) * 4,
        scratch_shapes=[
            pltpu.SMEM((tasks,), jnp.int32),
            pltpu.VMEM(acts.shape, acts.dtype),
            pltpu.VMEM((2 * rows, tokens), acts.dtype),
            pltpu.SemaphoreType.DMA((3,)),
        ],
        compiler_params=params(8),
        cost_estimate=pl.CostEstimate(
            flops=2 * tokens * tokens * depth, bytes_accessed=0, transcendentals=0
        ),
        name="prepare",
    )(order, acts, own)


def place(flat_ref, offset, mine_ref, other_ref):
    core = lax.axis_index("task_1")
    base = chip_at(offset) * 2
    side = 1 - core if offset in FLIP else core
    flat_ref[base + side] = mine_ref[...]
    flat_ref[base + 1 - side] = other_ref[...]


def chip_pair(flat_ref, rows_ref, outer, first, second):
    tokens = outer.shape[0]
    first_chip, second_chip = chip_at(first), chip_at(second)
    low = 2 * jnp.minimum(first_chip, second_chip)
    high = 2 * jnp.maximum(first_chip, second_chip)
    block = lax.dot_general(
        flat_ref[pl.ds(low, 2)].reshape(2 * tokens, -1), flat_ref[pl.ds(high, 2)].reshape(2 * tokens, -1),
        (((1,), (1,)), ((), ())), preferred_element_type=jnp.float32,
    )
    for a in range(2):
        for b in range(2):
            if first == second and b < a:
                continue
            pair = block[tokens * a : tokens * (a + 1), tokens * b : tokens * (b + 1)]
            row = jnp.sum(pair * outer, axis=0, keepdims=True)
            rows_ref[high + b, pl.ds(low + a, 1), :] = row
            if first != second or a != b:
                rows_ref[low + a, pl.ds(high + b, 1), :] = row


def early_kernel(*refs):
    outer_ref, flat_ref, rows_ref = refs[-3:]
    held = (0, *ORDER[:-1])
    for at, offset in enumerate(held):
        place(flat_ref, offset, refs[2 * at], refs[2 * at + 1])
    outer = outer_ref[...]
    for at, second in enumerate(held):
        for first in held[: at + 1]:
            chip_pair(flat_ref, rows_ref, outer, first, second)


def late_kernel(flat_in_ref, rows_in_ref, m2, o2, outer_ref, row_ref, flat_ref, rows_ref):
    chips = flat_ref.shape[0] // 2
    tasks = 2 * chips
    last = ORDER[-1]
    place(flat_ref, last, m2, o2)
    outer = outer_ref[...]
    for offset in (last, 0, *ORDER[:-1]):
        chip_pair(flat_ref, rows_ref, outer, last, offset)
    lane = lax.broadcasted_iota(jnp.int32, (tasks, LANES), 1)
    sub = lax.broadcasted_iota(jnp.int32, (tasks, LANES), 0)
    gram = jnp.zeros((tasks, LANES), jnp.float32)
    for j in range(tasks):
        total = jnp.sum(rows_ref[j], axis=1, keepdims=True)
        gram = jnp.where(lane == tasks * sub + j, total, gram)
    row_ref[...] = jnp.broadcast_to(jnp.sum(gram, axis=0, keepdims=True), row_ref.shape)


def partial_gram(mine, other, outer, copies):
    tokens, width = mine[0].shape
    tasks = 2 * len(mine)
    pair_flops = 8 * tokens * tokens * width
    held = (
        jax.ShapeDtypeStruct((tasks, tokens, width), jnp.bfloat16),
        jax.ShapeDtypeStruct((tasks, tasks, LANES), jnp.float32),
    )
    flat, rows = pl.pallas_call(
        early_kernel,
        out_shape=held,
        in_specs=[VMEM] * 7,
        out_specs=(VMEM, VMEM),
        compiler_params=params(8),
        cost_estimate=pl.CostEstimate(flops=6 * pair_flops, bytes_accessed=0, transcendentals=0),
        name="early_gram",
    )(*(block[offset] for offset in (0, *ORDER[:-1]) for block in (mine, other)), outer)
    row, _, _ = pl.pallas_call(
        late_kernel,
        out_shape=(jax.ShapeDtypeStruct((copies, LANES), jnp.float32), *held),
        in_specs=[VMEM] * 5,
        out_specs=(VMEM, VMEM, VMEM),
        input_output_aliases={0: 1, 1: 2},
        compiler_params=params(8),
        cost_estimate=pl.CostEstimate(flops=4 * pair_flops, bytes_accessed=0, transcendentals=0),
        name="late_gram",
    )(flat, rows, mine[ORDER[-1]], other[ORDER[-1]], outer)
    return row


def finish_kernel(*refs):
    chips = (len(refs) - 9) // 2
    turns_ref, grams_ref = refs[:2]
    mine, other = refs[2 : 2 + chips], refs[2 + chips : 2 + 2 * chips]
    acts_ref, update_ref, weights_ref, spread_ref, flat_ref, out_ref, sems = refs[-7:]
    core = lax.axis_index("task_1")
    _, width = mine[0].shape
    tasks = 2 * chips
    lane = lax.broadcasted_iota(jnp.int32, (tasks, LANES), 1)
    sub = lax.broadcasted_iota(jnp.int32, (tasks, LANES), 0)
    column_of = lane - tasks * sub
    gram = jnp.sum(grams_ref[...], axis=0, keepdims=True)
    gram = jnp.broadcast_to(gram, (tasks, LANES))
    mix = (lane == sub).astype(jnp.float32)
    steps = []
    for step in range(tasks):
        target = turns_ref[step]
        column = jnp.sum(jnp.where(column_of == target, gram, 0.0), axis=1, keepdims=True)
        column = jnp.broadcast_to(column, (tasks, LANES))
        scale = jnp.sum(jnp.where(sub == target, column, 0.0), axis=0, keepdims=True) + 1e-06
        steps.append((column, 1.0 / scale, (sub == target) & (lane != target)))
    for column, factor, touched in steps:
        dots = jnp.sum(mix * column, axis=0, keepdims=True)
        change = jnp.minimum(dots, 0.0) * factor
        mix = mix - jnp.where(touched, change, 0.0)
    weights = jnp.sum(jnp.where(lane < tasks, mix, 0.0), axis=1, keepdims=True)
    spread = jnp.broadcast_to(weights, (tasks, LANES))
    spread_ref[...] = spread
    flat_ref[...] = jnp.sum(jnp.where(lane == sub, spread, 0.0), axis=0)[:tasks]
    copies = [pltpu.make_async_copy(flat_ref, weights_ref, sems.at[0])]
    copies[0].start()
    terms = []
    for offset in range(chips):
        base = chip_at(offset) * 2
        side = 1 - core if offset in FLIP else core
        terms.append((spread_ref[pl.ds(base + side, 1), :], mine[offset]))
        terms.append((spread_ref[pl.ds(base + 1 - side, 1), :], other[offset]))
    for start in range(0, width, 256):
        size = min(256, width - start)
        blocks = []
        for at in range(start, start + size, LANES):
            total = None
            for factor, ref in terms:
                part = factor * ref[:, at : at + LANES].astype(jnp.float32)
                total = part if total is None else total + part
            blocks.append(total.astype(jnp.bfloat16))
        cols = pl.ds(start, size)
        out_ref[:, cols] = lax.dot_general(
            acts_ref[...], jnp.concatenate(blocks, axis=1), (((1,), (0,)), ((), ())),
            preferred_element_type=jnp.float32,
        )
        copy = pltpu.make_async_copy(out_ref.at[:, cols], update_ref.at[:, cols], sems.at[len(copies)])
        copy.start()
        copies.append(copy)
    for copy in copies:
        copy.wait()


def finish(turns, grams, mine, other, acts_rows):
    tokens, width = mine[0].shape
    tasks = 2 * len(mine)
    rows = acts_rows.shape[0]
    return pl.pallas_call(
        finish_kernel,
        out_shape=(
            jax.ShapeDtypeStruct((rows, width), jnp.float32),
            jax.ShapeDtypeStruct((tasks,), jnp.float32),
        ),
        in_specs=[VMEM] * (tasks + 3),
        out_specs=(pl.BlockSpec(memory_space=pl.ANY),) * 2,
        scratch_shapes=[
            pltpu.VMEM((tasks, LANES), jnp.float32),
            pltpu.VMEM((tasks,), jnp.float32),
            pltpu.VMEM((rows, width), jnp.float32),
            pltpu.SemaphoreType.DMA((1 + pl.cdiv(width, 256),)),
        ],
        compiler_params=params(8),
        cost_estimate=pl.CostEstimate(
            flops=2 * rows * tokens * width, bytes_accessed=4 * rows * width, transcendentals=0
        ),
        name="finish",
    )(turns, grams, *mine, *other, acts_rows)


def moved(value, offset):
    chips = lax.axis_size("task_0")
    pairs = [
        (2 * (chip ^ offset) + (1 - core if offset in FLIP else core), 2 * chip + core)
        for chip in range(chips)
        for core in range(2)
    ]
    return lax.ppermute(value, TASK, pairs)


def shards(acts, out_grads, order):
    mine, other = [out_grads[0]], []
    for offset in (1, 2, 3):
        mine.append(moved(mine[0], offset))
    for offset in (0, 1, 2, 3):
        other.append(lax.ppermute(mine[offset], "task_1", [(0, 1), (1, 0)]))
    outer, acts_rows, turns, held = prepare(order, acts, mine[0])
    mine[0] = held
    row = partial_gram(mine, other, outer, lax.axis_size(PARAM))
    grams = lax.all_to_all(row, PARAM, 0, 0, tiled=True, axis_index_groups=[[10, 0, 1, 2, 3, 4, 5, 6, 7, 8, 9, 11, 12, 13, 14, 15]])
    return finish(turns, grams, mine, other, acts_rows)


def solution(mesh):
    split = Mesh(mesh.devices.reshape(4, 2, 4, 4), ("task_0", "task_1", "param_0", "param_1"))
    placed = (P(), P(TASK, None, PARAM), P())
    return jax.shard_map(
        shards, mesh=split, in_specs=placed, out_specs=(P(TASK, PARAM), P()), check_vma=False
    )
```

profile of v0, /device:TPU:0, one launch (start us, length us, event | category | flops | bytes accessed | tf_op | source)
XLA Modules:
  0.0 32.8 jit_solution(10762404330200368699)
XLA Ops:
  0.6 1.7 %collective-permute-start.3 = (bf16[128,640]{1,0:T(8,128)(2,1)}, bf16[128,640]{1,0:T(8,128)(2,1)S(1)}, u32[]{:S(2)}, u32[]{:S(2)}) collective-permute-start(bf16[128,640]{1,0:T(8,128)(2,1)} %bitcast.5), channel_id=1, source_target_pairs={{32,0},{48,16},{0,32},{16,48},{96,64},{112,80},{64,96},{80,112},{3... | collective-permute-start | bytes 491528 | tf_op jit(solution)/shard_map/ppermute | solution.py:260
  2.3 2.1 %collective-permute-start.1 = (bf16[128,640]{1,0:T(8,128)(2,1)}, bf16[128,640]{1,0:T(8,128)(2,1)S(1)}, u32[]{:S(2)}, u32[]{:S(2)}) collective-permute-start(bf16[128,640]{1,0:T(8,128)(2,1)} %bitcast.6), channel_id=1, source_target_pairs={{96,0},{112,16},{64,32},{80,48},{32,64},{48,80},{0,96},{16,112},{9... | collective-permute-start | bytes 491528 | tf_op jit(solution)/shard_map/ppermute | solution.py:260
  4.4 0.0 collective-permute-start.5
  4.4 0.7 %collective-permute-start = (bf16[128,640]{1,0:T(8,128)(2,1)}, bf16[128,640]{1,0:T(8,128)(2,1)S(1)}, u32[]{:S(2)}, u32[]{:S(2)}) collective-permute-start(bf16[128,640]{1,0:T(8,128)(2,1)} %bitcast.8), channel_id=1, source_target_pairs={{0,16},{16,0},{1,17},{17,1},{2,18},{18,2},{3,19},{19,3},{4,20},{20... | collective-permute-start | bytes 491528 | tf_op jit(solution)/shard_map/ppermute | solution.py:268
  5.2 1.6 %collective-permute-done.3.refs_4_.refs_3_ = bf16[128,640]{1,0:T(8,128)(2,1)S(1)} collective-permute-done((bf16[128,640]{1,0:T(8,128)(2,1)}, bf16[128,640]{1,0:T(8,128)(2,1)S(1)}, u32[]{:S(2)}, u32[]{:S(2)}) %collective-permute-start.3) | collective-permute-done | bytes 163872 | tf_op jit(solution)/shard_map/ppermute | solution.py:260
  6.7 0.0 collective-permute-start.4
  6.7 6.2 %collective-permute-done.1.refs_2_.refs_5_ = bf16[128,640]{1,0:T(8,128)(2,1)S(1)} collective-permute-done((bf16[128,640]{1,0:T(8,128)(2,1)}, bf16[128,640]{1,0:T(8,128)(2,1)S(1)}, u32[]{:S(2)}, u32[]{:S(2)}) %collective-permute-start.1) | collective-permute-done | bytes 163872 | tf_op jit(solution)/shard_map/ppermute | solution.py:260
  12.9 0.0 collective-permute-start.2
  12.9 0.0 collective-permute-done.5.m2.refs_4_
  12.9 0.5 %collective-permute-start.6 = (bf16[128,640]{1,0:T(8,128)(2,1)S(1)}, bf16[128,640]{1,0:T(8,128)(2,1)S(1)}, u32[]{:S(2)}, u32[]{:S(2)}) collective-permute-start(bf16[128,640]{1,0:T(8,128)(2,1)S(1)} %collective-permute-done.5.m2.refs_4_), channel_id=1, source_target_pairs={{0,16},{16,0},{1,17},{17,1},{2,18},{18,2},{3,19},{19,3},{4,20},{20... | collective-permute-start | bytes 491528 | tf_op jit(solution)/shard_map/ppermute | solution.py:268
  13.4 0.0 copy-start
  13.4 1.2 %copy-done = bf16[128,3584]{1,0:T(8,128)(2,1)S(1)} copy-done((bf16[128,3584]{1,0:T(8,128)(2,1)S(1)}, bf16[128,3584]{1,0:T(8,128)(2,1)}, u32[]{:S(2)}) %copy-start) | copy-done | bytes 917528
  14.6 0.0 copy-start.1
  14.6 0.9 %copy-done.1 = bf16[1,128,640]{2,1,0:T(8,128)(2,1)S(1)} copy-done((bf16[1,128,640]{2,1,0:T(8,128)(2,1)S(1)}, bf16[1,128,640]{2,1,0:T(8,128)(2,1)}, u32[]{:S(2)}) %copy-start.1) | copy-done | bytes 163864
  15.5 0.0 copy-start.2
  15.5 0.7 %copy-done.2 = s32[8]{0:T(128)S(1)} copy-done((s32[8]{0:T(128)S(1)}, s32[8]{0:T(128)}, u32[]{:S(2)}) %copy-start.2) | copy-done | bytes 56
  16.2 0.9 %prepare.1 = (f32[128,128]{1,0:T(8,128)S(1)}, bf16[448,128]{1,0:T(8,128)(2,1)S(1)}, s32[8,8,128]{2,1,0:T(8,128)S(1)}, bf16[128,640]{1,0:T(8,128)(2,1)S(1)}) custom-call(s32[8]{0:T(128)S(1)} %copy-done.2, bf16[128,3584]{1,0:T(8,128)(2,1)S(1)} %copy-done, bf16[128,640]{1,0:T(8,128)(2,1)S(1)} %bitcast.9), custom_call_target="tpu_custom_call" | custom-call | flops 117440512 | tf_op jit(solution)/shard_map/prepare/pallas_call | solution.py:59
  17.1 0.0 collective-permute-done.refs_1_.refs_6_
  17.1 0.0 collective-permute-done.4.refs_5_.refs_7_
  17.1 0.0 collective-permute-done.2.refs_3_.refs_9_
  17.1 0.9 %early_gram.1 = (bf16[8,128,640]{2,1,0:T(8,128)(2,1)S(1)}, f32[8,8,128]{2,1,0:T(8,128)S(1)}) custom-call(bf16[128,640]{1,0:T(8,128)(2,1)S(1)} %get-tuple-element.10.refs_0_.refs_2_, bf16[128,640]{1,0:T(8,128)(2,1)S(1)} %collective-permute-done.refs_1_.refs_6_, bf16[128,640]{1,0:T(8,128)(2,1)S(1)} %collective-permute-done.1.refs_2_.refs_5_, ...), custom_call_target="tpu_custom_call" | custom-call | flops 503316480 | tf_op jit(solution)/shard_map/early_gram/pallas_call | solution.py:147
  18.0 0.0 collective-permute-done.6.o2.refs_8_
  18.0 0.8 %late_gram.1 = (f32[16,128]{1,0:T(8,128)S(1)}, bf16[8,128,640]{2,1,0:T(8,128)(2,1)S(1)}, f32[8,8,128]{2,1,0:T(8,128)S(1)}) custom-call(bf16[8,128,640]{2,1,0:T(8,128)(2,1)S(1)} %get-tuple-element.12.flat_in_ref, f32[8,8,128]{2,1,0:T(8,128)S(1)} %get-tuple-element.13.rows_in_ref, ...), custom_call_target="tpu_custom_call", output_to_operand_aliasing={{1}: (0, {}), {2}: (1, {})} | custom-call | flops 335544320 | tf_op jit(solution)/shard_map/late_gram/pallas_call | solution.py:156
  18.8 12.3 %all_to_all.11 = f32[16,1,128]{2,1,0:T(1,128)S(1)} all-to-all(f32[16,1,128]{2,1,0:T(1,128)S(1)} %bitcast.11), channel_id=1, replica_groups={{10,0,1,2,3,4,5,6,7,8,9,11,12,13,14,15},{26,16,17,18,19,20,21,22,23,24,..., dimensions={0} | all-to-all | bytes 16384 | tf_op jit(solution)/shard_map/all_to_all | solution.py:272
  31.1 1.7 %finish.1 = (f32[448,640]{1,0:T(8,128)}, f32[8]{0:T(128)}) custom-call(s32[8,8,128]{2,1,0:T(8,128)S(1)} %get-tuple-element.9.refs_0_, f32[16,128]{1,0:T(8,128)S(1)} %bitcast.10, bf16[128,640]{1,0:T(8,128)(2,1)S(1)} %get-tuple-element.10.refs_0_.refs_2_, bf16[128,640]{1,0:T(8,128)(2,1)S(1)} %collective-permute-done.3.refs_4_.refs_3_, ...), custom_call_target="tpu_custom_call" | custom-call | flops 73400320 | bytes 1146880 | tf_op jit(solution)/shard_map/finish/pallas_call | solution.py:231
Async XLA Ops:
  0.6 6.1 %collective-permute-start.3 = (bf16[128,640]{1,0:T(8,128)(2,1)}, bf16[128,640]{1,0:T(8,128)(2,1)S(1)}, u32[]{:S(2)}, u32[]{:S(2)}) collective-permute-start(bf16[128,640]{1,0:T(8,128)(2,1)} %bitcast.5), channel_id=1, source_target_pairs={{32,0},{48,16},{0,32},{16,48},{96,64},{112,80},{64,96},{80,112},{3... | collective-permute-start | bytes 491528 | tf_op jit(solution)/shard_map/ppermute | solution.py:260
  2.3 10.6 %collective-permute-start.1 = (bf16[128,640]{1,0:T(8,128)(2,1)}, bf16[128,640]{1,0:T(8,128)(2,1)S(1)}, u32[]{:S(2)}, u32[]{:S(2)}) collective-permute-start(bf16[128,640]{1,0:T(8,128)(2,1)} %bitcast.6), channel_id=1, source_target_pairs={{96,0},{112,16},{64,32},{80,48},{32,64},{48,80},{0,96},{16,112},{9... | collective-permute-start | bytes 491528 | tf_op jit(solution)/shard_map/ppermute | solution.py:260
  4.4 8.5 %collective-permute-start.5 = (bf16[128,640]{1,0:T(8,128)(2,1)}, bf16[128,640]{1,0:T(8,128)(2,1)S(1)}, u32[]{:S(2)}, u32[]{:S(2)}) collective-permute-start(bf16[128,640]{1,0:T(8,128)(2,1)} %bitcast.7), channel_id=1, source_target_pairs={{80,0},{64,16},{112,32},{96,48},{16,64},{0,80},{48,96},{32,112},{8... | collective-permute-start | bytes 491528 | tf_op jit(solution)/shard_map/ppermute | solution.py:260
  4.4 12.7 %collective-permute-start = (bf16[128,640]{1,0:T(8,128)(2,1)}, bf16[128,640]{1,0:T(8,128)(2,1)S(1)}, u32[]{:S(2)}, u32[]{:S(2)}) collective-permute-start(bf16[128,640]{1,0:T(8,128)(2,1)} %bitcast.8), channel_id=1, source_target_pairs={{0,16},{16,0},{1,17},{17,1},{2,18},{18,2},{3,19},{19,3},{4,20},{20... | collective-permute-start | bytes 491528 | tf_op jit(solution)/shard_map/ppermute | solution.py:268
  6.7 10.4 %collective-permute-start.4 = (bf16[128,640]{1,0:T(8,128)(2,1)S(1)}, bf16[128,640]{1,0:T(8,128)(2,1)S(1)}, u32[]{:S(2)}, u32[]{:S(2)}) collective-permute-start(bf16[128,640]{1,0:T(8,128)(2,1)S(1)} %collective-permute-done.3.refs_4_.refs_3_), channel_id=1, source_target_pairs={{0,16},{16,0},{1,17},{17,1},{2,18},{18,2},{3,19},{19,3},{4,20},{20... | collective-permute-start | bytes 491528 | tf_op jit(solution)/shard_map/ppermute | solution.py:268
  12.9 4.2 %collective-permute-start.2 = (bf16[128,640]{1,0:T(8,128)(2,1)S(1)}, bf16[128,640]{1,0:T(8,128)(2,1)S(1)}, u32[]{:S(2)}, u32[]{:S(2)}) collective-permute-start(bf16[128,640]{1,0:T(8,128)(2,1)S(1)} %collective-permute-done.1.refs_2_.refs_5_), channel_id=1, source_target_pairs={{0,16},{16,0},{1,17},{17,1},{2,18},{18,2},{3,19},{19,3},{4,20},{20... | collective-permute-start | bytes 491528 | tf_op jit(solution)/shard_map/ppermute | solution.py:268
  12.9 5.1 %collective-permute-start.6 = (bf16[128,640]{1,0:T(8,128)(2,1)S(1)}, bf16[128,640]{1,0:T(8,128)(2,1)S(1)}, u32[]{:S(2)}, u32[]{:S(2)}) collective-permute-start(bf16[128,640]{1,0:T(8,128)(2,1)S(1)} %collective-permute-done.5.m2.refs_4_), channel_id=1, source_target_pairs={{0,16},{16,0},{1,17},{17,1},{2,18},{18,2},{3,19},{19,3},{4,20},{20... | collective-permute-start | bytes 491528 | tf_op jit(solution)/shard_map/ppermute | solution.py:268
  13.4 1.2 %copy-start = (bf16[128,3584]{1,0:T(8,128)(2,1)S(1)}, bf16[128,3584]{1,0:T(8,128)(2,1)}, u32[]{:S(2)}) copy-start(bf16[128,3584]{1,0:T(8,128)(2,1)} %acts_hbm.1) | copy-start | bytes 2752516
  14.6 0.9 %copy-start.1 = (bf16[1,128,640]{2,1,0:T(8,128)(2,1)S(1)}, bf16[1,128,640]{2,1,0:T(8,128)(2,1)}, u32[]{:S(2)}) copy-start(bf16[1,128,640]{2,1,0:T(8,128)(2,1)} %param.4) | copy-start | bytes 491524
  15.5 0.7 %copy-start.2 = (s32[8]{0:T(128)S(1)}, s32[8]{0:T(128)}, u32[]{:S(2)}) copy-start(s32[8]{0:T(128)} %order_hbm.1) | copy-start | bytes 100
where the time goes:
time: 33 us; the launch traced here: 32.8 us
  blocking collectives  12.3 us (37%)
  waiting for transfers between devices  7.75 us (23%)
  starting transfers between devices  5.04 us (15%)
  Pallas kernels  4.24 us (13%)
  local copies, waits for them, and re-layouts  2.75 us (8%)
  between operations  0.69 us (2%)
    all_to_all x1, blocking collectives, shards(): lax.all_to_all(row, PARAM, 0, 0, tiled=True, axis_index_groups=[[10, 0, 1...  12.3 us
    ppermute x3, waiting for transfers between devices, moved(): return lax.ppermute(value, TASK, pairs)  7.74 us
    ppermute x3, starting transfers between devices, moved(): return lax.ppermute(value, TASK, pairs)  3.78 us
    unnamed x6, local copies, waits for them, and re-layouts  2.75 us
    pallas_call x1, Pallas kernels, finish(): pl.pallas_call(finish_kernel, out_shape=(jax.ShapeDtypeStruct((rows, widt...  1.69 us
    ppermute x4, starting transfers between devices, shards(): other.append(lax.ppermute(mine[offset], 'task_1', [(0, 1), (1, 0)]))  1.26 us
    pallas_call x1, Pallas kernels, partial_gram(): pl.pallas_call(early_kernel, out_shape=held, in_specs=[VMEM] * 7, out_spe...  0.91 us
    pallas_call x1, Pallas kernels, prepare(): pl.pallas_call(prepare_kernel, out_shape=(jax.ShapeDtypeStruct((tokens, t...  0.89 us
  transfers between devices with their start and end apart: 7, of which 2 were waited for; matrix products, arithmetic and copies ran while one was open for 0% of the time, Pallas kernels for 6%

commit v1 on v0

--- a/solution.py
+++ b/solution.py
@@ -125,7 +125,7 @@
     last = ORDER[-1]
     place(flat_ref, last, m2, o2)
     outer = outer_ref[...]
-    for offset in (last, 0, *ORDER[:-1]):
+    for offset in (0, *ORDER[:-1], last):
         chip_pair(flat_ref, rows_ref, outer, last, offset)
     lane = lax.broadcasted_iota(jnp.int32, (tasks, LANES), 1)
     sub = lax.broadcasted_iota(jnp.int32, (tasks, LANES), 0)
@@ -196,7 +196,6 @@
     spread_ref[...] = spread
     flat_ref[...] = jnp.sum(jnp.where(lane == sub, spread, 0.0), axis=0)[:tasks]
     copies = [pltpu.make_async_copy(flat_ref, weights_ref, sems.at[0])]
-    copies[0].start()
     terms = []
     for offset in range(chips):
         base = chip_at(offset) * 2
@@ -220,6 +219,7 @@
         copy = pltpu.make_async_copy(out_ref.at[:, cols], update_ref.at[:, cols], sems.at[len(copies)])
         copy.start()
         copies.append(copy)
+    copies[0].start()
     for copy in copies:
         copy.wait()
 
@@ -260,6 +260,12 @@
     return lax.ppermute(value, TASK, pairs)
 
 
+def farthest_first():
+    rows, columns = lax.axis_size(PARAM[0]), lax.axis_size(PARAM[1])
+    farthest = rows // 2 * columns + columns // 2
+    return [farthest] + [chip for chip in range(rows * columns) if chip != farthest]
+
+
 def shards(acts, out_grads, order):
     mine, other = [out_grads[0]], []
     for offset in (1, 2, 3):
@@ -269,7 +275,7 @@
     outer, acts_rows, turns, held = prepare(order, acts, mine[0])
     mine[0] = held
     row = partial_gram(mine, other, outer, lax.axis_size(PARAM))
-    grams = lax.all_to_all(row, PARAM, 0, 0, tiled=True, axis_index_groups=[[10, 0, 1, 2, 3, 4, 5, 6, 7, 8, 9, 11, 12, 13, 14, 15]])
+    grams = lax.all_to_all(row, PARAM, 0, 0, tiled=True, axis_index_groups=[farthest_first()])
     return finish(turns, grams, mine, other, acts_rows)
 
 

time: 33 us -> 33 us (level)
  no operation moved by 1% of the time
where the time goes in v1:
time: 33 us; the launch traced here: 32.8 us
  blocking collectives  12.3 us (37%)
  waiting for transfers between devices  7.75 us (23%)
  starting transfers between devices  5.04 us (15%)
  Pallas kernels  4.24 us (13%)
  local copies, waits for them, and re-layouts  2.75 us (8%)
  between operations  0.69 us (2%)
    all_to_all x1, blocking collectives, shards(): lax.all_to_all(row, PARAM, 0, 0, tiled=True, axis_index_groups=[farthest_...  12.3 us
    ppermute x3, waiting for transfers between devices, moved(): return lax.ppermute(value, TASK, pairs)  7.74 us
    ppermute x3, starting transfers between devices, moved(): return lax.ppermute(value, TASK, pairs)  3.78 us
    unnamed x6, local copies, waits for them, and re-layouts  2.75 us
    pallas_call x1, Pallas kernels, finish(): pl.pallas_call(finish_kernel, out_shape=(jax.ShapeDtypeStruct((rows, widt...  1.69 us
    ppermute x4, starting transfers between devices, shards(): other.append(lax.ppermute(mine[offset], 'task_1', [(0, 1), (1, 0)]))  1.26 us
    pallas_call x1, Pallas kernels, partial_gram(): pl.pallas_call(early_kernel, out_shape=held, in_specs=[VMEM] * 7, out_spe...  0.91 us
    pallas_call x1, Pallas kernels, prepare(): pl.pallas_call(prepare_kernel, out_shape=(jax.ShapeDtypeStruct((tokens, t...  0.89 us
  transfers between devices with their start and end apart: 7, of which 2 were waited for; matrix products, arithmetic and copies ran while one was open for 0% of the time, Pallas kernels for 6%

profile of v1, /device:TPU:0, one launch (start us, length us, event | category | flops | bytes accessed | tf_op | source)
XLA Modules:
  0.0 32.8 jit_solution(4031530965179020472)
XLA Ops:
  0.6 1.7 %collective-permute-start.3 = (bf16[128,640]{1,0:T(8,128)(2,1)}, bf16[128,640]{1,0:T(8,128)(2,1)S(1)}, u32[]{:S(2)}, u32[]{:S(2)}) collective-permute-start(bf16[128,640]{1,0:T(8,128)(2,1)} %bitcast.5), channel_id=1, source_target_pairs={{32,0},{48,16},{0,32},{16,48},{96,64},{112,80},{64,96},{80,112},{3... | collective-permute-start | bytes 491528 | tf_op jit(solution)/shard_map/ppermute | solution.py:260
  2.3 2.1 %collective-permute-start.1 = (bf16[128,640]{1,0:T(8,128)(2,1)}, bf16[128,640]{1,0:T(8,128)(2,1)S(1)}, u32[]{:S(2)}, u32[]{:S(2)}) collective-permute-start(bf16[128,640]{1,0:T(8,128)(2,1)} %bitcast.6), channel_id=1, source_target_pairs={{96,0},{112,16},{64,32},{80,48},{32,64},{48,80},{0,96},{16,112},{9... | collective-permute-start | bytes 491528 | tf_op jit(solution)/shard_map/ppermute | solution.py:260
  4.4 0.0 collective-permute-start.5
  4.4 0.7 %collective-permute-start = (bf16[128,640]{1,0:T(8,128)(2,1)}, bf16[128,640]{1,0:T(8,128)(2,1)S(1)}, u32[]{:S(2)}, u32[]{:S(2)}) collective-permute-start(bf16[128,640]{1,0:T(8,128)(2,1)} %bitcast.8), channel_id=1, source_target_pairs={{0,16},{16,0},{1,17},{17,1},{2,18},{18,2},{3,19},{19,3},{4,20},{20... | collective-permute-start | bytes 491528 | tf_op jit(solution)/shard_map/ppermute | solution.py:274
  5.2 1.6 %collective-permute-done.3.refs_4_.refs_3_ = bf16[128,640]{1,0:T(8,128)(2,1)S(1)} collective-permute-done((bf16[128,640]{1,0:T(8,128)(2,1)}, bf16[128,640]{1,0:T(8,128)(2,1)S(1)}, u32[]{:S(2)}, u32[]{:S(2)}) %collective-permute-start.3) | collective-permute-done | bytes 163872 | tf_op jit(solution)/shard_map/ppermute | solution.py:260
  6.7 0.0 collective-permute-start.4
  6.7 6.2 %collective-permute-done.1.refs_2_.refs_5_ = bf16[128,640]{1,0:T(8,128)(2,1)S(1)} collective-permute-done((bf16[128,640]{1,0:T(8,128)(2,1)}, bf16[128,640]{1,0:T(8,128)(2,1)S(1)}, u32[]{:S(2)}, u32[]{:S(2)}) %collective-permute-start.1) | collective-permute-done | bytes 163872 | tf_op jit(solution)/shard_map/ppermute | solution.py:260
  12.9 0.0 collective-permute-start.2
  12.9 0.0 collective-permute-done.5.m2.refs_4_
  12.9 0.5 %collective-permute-start.6 = (bf16[128,640]{1,0:T(8,128)(2,1)S(1)}, bf16[128,640]{1,0:T(8,128)(2,1)S(1)}, u32[]{:S(2)}, u32[]{:S(2)}) collective-permute-start(bf16[128,640]{1,0:T(8,128)(2,1)S(1)} %collective-permute-done.5.m2.refs_4_), channel_id=1, source_target_pairs={{0,16},{16,0},{1,17},{17,1},{2,18},{18,2},{3,19},{19,3},{4,20},{20... | collective-permute-start | bytes 491528 | tf_op jit(solution)/shard_map/ppermute | solution.py:274
  13.4 0.0 copy-start
  13.4 1.2 %copy-done = bf16[128,3584]{1,0:T(8,128)(2,1)S(1)} copy-done((bf16[128,3584]{1,0:T(8,128)(2,1)S(1)}, bf16[128,3584]{1,0:T(8,128)(2,1)}, u32[]{:S(2)}) %copy-start) | copy-done | bytes 917528
  14.6 0.0 copy-start.1
  14.6 0.9 %copy-done.1 = bf16[1,128,640]{2,1,0:T(8,128)(2,1)S(1)} copy-done((bf16[1,128,640]{2,1,0:T(8,128)(2,1)S(1)}, bf16[1,128,640]{2,1,0:T(8,128)(2,1)}, u32[]{:S(2)}) %copy-start.1) | copy-done | bytes 163864
  15.5 0.0 copy-start.2
  15.5 0.7 %copy-done.2 = s32[8]{0:T(128)S(1)} copy-done((s32[8]{0:T(128)S(1)}, s32[8]{0:T(128)}, u32[]{:S(2)}) %copy-start.2) | copy-done | bytes 56
  16.2 0.9 %prepare.1 = (f32[128,128]{1,0:T(8,128)S(1)}, bf16[448,128]{1,0:T(8,128)(2,1)S(1)}, s32[8,8,128]{2,1,0:T(8,128)S(1)}, bf16[128,640]{1,0:T(8,128)(2,1)S(1)}) custom-call(s32[8]{0:T(128)S(1)} %copy-done.2, bf16[128,3584]{1,0:T(8,128)(2,1)S(1)} %copy-done, bf16[128,640]{1,0:T(8,128)(2,1)S(1)} %bitcast.9), custom_call_target="tpu_custom_call" | custom-call | flops 117440512 | tf_op jit(solution)/shard_map/prepare/pallas_call | solution.py:59
  17.1 0.0 collective-permute-done.refs_1_.refs_6_
  17.1 0.0 collective-permute-done.4.refs_5_.refs_7_
  17.1 0.0 collective-permute-done.2.refs_3_.refs_9_
  17.1 0.9 %early_gram.1 = (bf16[8,128,640]{2,1,0:T(8,128)(2,1)S(1)}, f32[8,8,128]{2,1,0:T(8,128)S(1)}) custom-call(bf16[128,640]{1,0:T(8,128)(2,1)S(1)} %get-tuple-element.10.refs_0_.refs_2_, bf16[128,640]{1,0:T(8,128)(2,1)S(1)} %collective-permute-done.refs_1_.refs_6_, bf16[128,640]{1,0:T(8,128)(2,1)S(1)} %collective-permute-done.1.refs_2_.refs_5_, ...), custom_call_target="tpu_custom_call" | custom-call | flops 503316480 | tf_op jit(solution)/shard_map/early_gram/pallas_call | solution.py:147
  18.0 0.0 collective-permute-done.6.o2.refs_8_
  18.0 0.7 %late_gram.1 = (f32[16,128]{1,0:T(8,128)S(1)}, bf16[8,128,640]{2,1,0:T(8,128)(2,1)S(1)}, f32[8,8,128]{2,1,0:T(8,128)S(1)}) custom-call(bf16[8,128,640]{2,1,0:T(8,128)(2,1)S(1)} %get-tuple-element.12.flat_in_ref, f32[8,8,128]{2,1,0:T(8,128)S(1)} %get-tuple-element.13.rows_in_ref, ...), custom_call_target="tpu_custom_call", output_to_operand_aliasing={{1}: (0, {}), {2}: (1, {})} | custom-call | flops 335544320 | tf_op jit(solution)/shard_map/late_gram/pallas_call | solution.py:156
  18.8 12.3 %all_to_all.11 = f32[16,1,128]{2,1,0:T(1,128)S(1)} all-to-all(f32[16,1,128]{2,1,0:T(1,128)S(1)} %bitcast.11), channel_id=1, replica_groups={{10,0,1,2,3,4,5,6,7,8,9,11,12,13,14,15},{26,16,17,18,19,20,21,22,23,24,..., dimensions={0} | all-to-all | bytes 16384 | tf_op jit(solution)/shard_map/all_to_all | solution.py:278
  31.1 1.7 %finish.1 = (f32[448,640]{1,0:T(8,128)}, f32[8]{0:T(128)}) custom-call(s32[8,8,128]{2,1,0:T(8,128)S(1)} %get-tuple-element.9.refs_0_, f32[16,128]{1,0:T(8,128)S(1)} %bitcast.10, bf16[128,640]{1,0:T(8,128)(2,1)S(1)} %get-tuple-element.10.refs_0_.refs_2_, bf16[128,640]{1,0:T(8,128)(2,1)S(1)} %collective-permute-done.3.refs_4_.refs_3_, ...), custom_call_target="tpu_custom_call" | custom-call | flops 73400320 | bytes 1146880 | tf_op jit(solution)/shard_map/finish/pallas_call | solution.py:231
Async XLA Ops:
  0.6 6.1 %collective-permute-start.3 = (bf16[128,640]{1,0:T(8,128)(2,1)}, bf16[128,640]{1,0:T(8,128)(2,1)S(1)}, u32[]{:S(2)}, u32[]{:S(2)}) collective-permute-start(bf16[128,640]{1,0:T(8,128)(2,1)} %bitcast.5), channel_id=1, source_target_pairs={{32,0},{48,16},{0,32},{16,48},{96,64},{112,80},{64,96},{80,112},{3... | collective-permute-start | bytes 491528 | tf_op jit(solution)/shard_map/ppermute | solution.py:260
  2.3 10.6 %collective-permute-start.1 = (bf16[128,640]{1,0:T(8,128)(2,1)}, bf16[128,640]{1,0:T(8,128)(2,1)S(1)}, u32[]{:S(2)}, u32[]{:S(2)}) collective-permute-start(bf16[128,640]{1,0:T(8,128)(2,1)} %bitcast.6), channel_id=1, source_target_pairs={{96,0},{112,16},{64,32},{80,48},{32,64},{48,80},{0,96},{16,112},{9... | collective-permute-start | bytes 491528 | tf_op jit(solution)/shard_map/ppermute | solution.py:260
  4.4 8.5 %collective-permute-start.5 = (bf16[128,640]{1,0:T(8,128)(2,1)}, bf16[128,640]{1,0:T(8,128)(2,1)S(1)}, u32[]{:S(2)}, u32[]{:S(2)}) collective-permute-start(bf16[128,640]{1,0:T(8,128)(2,1)} %bitcast.7), channel_id=1, source_target_pairs={{80,0},{64,16},{112,32},{96,48},{16,64},{0,80},{48,96},{32,112},{8... | collective-permute-start | bytes 491528 | tf_op jit(solution)/shard_map/ppermute | solution.py:260
  4.4 12.7 %collective-permute-start = (bf16[128,640]{1,0:T(8,128)(2,1)}, bf16[128,640]{1,0:T(8,128)(2,1)S(1)}, u32[]{:S(2)}, u32[]{:S(2)}) collective-permute-start(bf16[128,640]{1,0:T(8,128)(2,1)} %bitcast.8), channel_id=1, source_target_pairs={{0,16},{16,0},{1,17},{17,1},{2,18},{18,2},{3,19},{19,3},{4,20},{20... | collective-permute-start | bytes 491528 | tf_op jit(solution)/shard_map/ppermute | solution.py:274
  6.7 10.4 %collective-permute-start.4 = (bf16[128,640]{1,0:T(8,128)(2,1)S(1)}, bf16[128,640]{1,0:T(8,128)(2,1)S(1)}, u32[]{:S(2)}, u32[]{:S(2)}) collective-permute-start(bf16[128,640]{1,0:T(8,128)(2,1)S(1)} %collective-permute-done.3.refs_4_.refs_3_), channel_id=1, source_target_pairs={{0,16},{16,0},{1,17},{17,1},{2,18},{18,2},{3,19},{19,3},{4,20},{20... | collective-permute-start | bytes 491528 | tf_op jit(solution)/shard_map/ppermute | solution.py:274
  12.9 4.2 %collective-permute-start.2 = (bf16[128,640]{1,0:T(8,128)(2,1)S(1)}, bf16[128,640]{1,0:T(8,128)(2,1)S(1)}, u32[]{:S(2)}, u32[]{:S(2)}) collective-permute-start(bf16[128,640]{1,0:T(8,128)(2,1)S(1)} %collective-permute-done.1.refs_2_.refs_5_), channel_id=1, source_target_pairs={{0,16},{16,0},{1,17},{17,1},{2,18},{18,2},{3,19},{19,3},{4,20},{20... | collective-permute-start | bytes 491528 | tf_op jit(solution)/shard_map/ppermute | solution.py:274
  12.9 5.1 %collective-permute-start.6 = (bf16[128,640]{1,0:T(8,128)(2,1)S(1)}, bf16[128,640]{1,0:T(8,128)(2,1)S(1)}, u32[]{:S(2)}, u32[]{:S(2)}) collective-permute-start(bf16[128,640]{1,0:T(8,128)(2,1)S(1)} %collective-permute-done.5.m2.refs_4_), channel_id=1, source_target_pairs={{0,16},{16,0},{1,17},{17,1},{2,18},{18,2},{3,19},{19,3},{4,20},{20... | collective-permute-start | bytes 491528 | tf_op jit(solution)/shard_map/ppermute | solution.py:274
  13.4 1.2 %copy-start = (bf16[128,3584]{1,0:T(8,128)(2,1)S(1)}, bf16[128,3584]{1,0:T(8,128)(2,1)}, u32[]{:S(2)}) copy-start(bf16[128,3584]{1,0:T(8,128)(2,1)} %acts_hbm.1) | copy-start | bytes 2752516
  14.6 0.9 %copy-start.1 = (bf16[1,128,640]{2,1,0:T(8,128)(2,1)S(1)}, bf16[1,128,640]{2,1,0:T(8,128)(2,1)}, u32[]{:S(2)}) copy-start(bf16[1,128,640]{2,1,0:T(8,128)(2,1)} %param.4) | copy-start | bytes 491524
  15.5 0.7 %copy-start.2 = (s32[8]{0:T(128)S(1)}, s32[8]{0:T(128)}, u32[]{:S(2)}) copy-start(s32[8]{0:T(128)} %order_hbm.1) | copy-start | bytes 100

commit v2 on v1

--- a/solution.py
+++ b/solution.py
@@ -125,7 +125,7 @@
     last = ORDER[-1]
     place(flat_ref, last, m2, o2)
     outer = outer_ref[...]
-    for offset in (0, *ORDER[:-1], last):
+    for offset in (last, 0, *ORDER[:-1]):
         chip_pair(flat_ref, rows_ref, outer, last, offset)
     lane = lax.broadcasted_iota(jnp.int32, (tasks, LANES), 1)
     sub = lax.broadcasted_iota(jnp.int32, (tasks, LANES), 0)
@@ -159,7 +159,7 @@
         in_specs=[VMEM] * 5,
         out_specs=(VMEM, VMEM, VMEM),
         input_output_aliases={0: 1, 1: 2},
-        compiler_params=params(8),
+        compiler_params=pltpu.CompilerParams(vmem_limit_bytes=8 << 20),
         cost_estimate=pl.CostEstimate(flops=4 * pair_flops, bytes_accessed=0, transcendentals=0),
         name="late_gram",
     )(flat, rows, mine[ORDER[-1]], other[ORDER[-1]], outer)
@@ -242,7 +242,7 @@
             pltpu.VMEM((rows, width), jnp.float32),
             pltpu.SemaphoreType.DMA((1 + pl.cdiv(width, 256),)),
         ],
-        compiler_params=params(8),
+        compiler_params=pltpu.CompilerParams(vmem_limit_bytes=8 << 20),
         cost_estimate=pl.CostEstimate(
             flops=2 * rows * tokens * width, bytes_accessed=4 * rows * width, transcendentals=0
         ),

time: 33 us -> 33 us (level)
  no operation moved by 1% of the time
where the time goes in v2:
time: 33 us; the launch traced here: 32.8 us
  blocking collectives  12.3 us (37%)
  waiting for transfers between devices  7.75 us (23%)
  starting transfers between devices  5.04 us (15%)
  Pallas kernels  4.24 us (13%)
  local copies, waits for them, and re-layouts  2.75 us (8%)
  between operations  0.69 us (2%)
    all_to_all x1, blocking collectives, shards(): lax.all_to_all(row, PARAM, 0, 0, tiled=True, axis_index_groups=[farthest_...  12.3 us
    ppermute x3, waiting for transfers between devices, moved(): return lax.ppermute(value, TASK, pairs)  7.74 us
    ppermute x3, starting transfers between devices, moved(): return lax.ppermute(value, TASK, pairs)  3.78 us
    unnamed x6, local copies, waits for them, and re-layouts  2.75 us
    pallas_call x1, Pallas kernels, finish(): pl.pallas_call(finish_kernel, out_shape=(jax.ShapeDtypeStruct((rows, widt...  1.69 us
    ppermute x4, starting transfers between devices, shards(): other.append(lax.ppermute(mine[offset], 'task_1', [(0, 1), (1, 0)]))  1.26 us
    pallas_call x1, Pallas kernels, partial_gram(): pl.pallas_call(early_kernel, out_shape=held, in_specs=[VMEM] * 7, out_spe...  0.91 us
    pallas_call x1, Pallas kernels, prepare(): pl.pallas_call(prepare_kernel, out_shape=(jax.ShapeDtypeStruct((tokens, t...  0.89 us
  transfers between devices with their start and end apart: 7, of which 2 were waited for; matrix products, arithmetic and copies ran while one was open for 0% of the time, Pallas kernels for 6%

profile of v2, /device:TPU:0, one launch (start us, length us, event | category | flops | bytes accessed | tf_op | source)
XLA Modules:
  0.0 32.8 jit_solution(10159627332260714759)
XLA Ops:
  0.6 1.7 %collective-permute-start.3 = (bf16[128,640]{1,0:T(8,128)(2,1)}, bf16[128,640]{1,0:T(8,128)(2,1)S(1)}, u32[]{:S(2)}, u32[]{:S(2)}) collective-permute-start(bf16[128,640]{1,0:T(8,128)(2,1)} %bitcast.5), channel_id=1, source_target_pairs={{32,0},{48,16},{0,32},{16,48},{96,64},{112,80},{64,96},{80,112},{3... | collective-permute-start | bytes 491528 | tf_op jit(solution)/shard_map/ppermute | solution.py:260
  2.3 2.1 %collective-permute-start.1 = (bf16[128,640]{1,0:T(8,128)(2,1)}, bf16[128,640]{1,0:T(8,128)(2,1)S(1)}, u32[]{:S(2)}, u32[]{:S(2)}) collective-permute-start(bf16[128,640]{1,0:T(8,128)(2,1)} %bitcast.6), channel_id=1, source_target_pairs={{96,0},{112,16},{64,32},{80,48},{32,64},{48,80},{0,96},{16,112},{9... | collective-permute-start | bytes 491528 | tf_op jit(solution)/shard_map/ppermute | solution.py:260
  4.4 0.0 collective-permute-start.5
  4.4 0.7 %collective-permute-start = (bf16[128,640]{1,0:T(8,128)(2,1)}, bf16[128,640]{1,0:T(8,128)(2,1)S(1)}, u32[]{:S(2)}, u32[]{:S(2)}) collective-permute-start(bf16[128,640]{1,0:T(8,128)(2,1)} %bitcast.8), channel_id=1, source_target_pairs={{0,16},{16,0},{1,17},{17,1},{2,18},{18,2},{3,19},{19,3},{4,20},{20... | collective-permute-start | bytes 491528 | tf_op jit(solution)/shard_map/ppermute | solution.py:274
  5.2 1.6 %collective-permute-done.3.refs_4_.refs_3_ = bf16[128,640]{1,0:T(8,128)(2,1)S(1)} collective-permute-done((bf16[128,640]{1,0:T(8,128)(2,1)}, bf16[128,640]{1,0:T(8,128)(2,1)S(1)}, u32[]{:S(2)}, u32[]{:S(2)}) %collective-permute-start.3) | collective-permute-done | bytes 163872 | tf_op jit(solution)/shard_map/ppermute | solution.py:260
  6.7 0.0 collective-permute-start.4
  6.7 6.2 %collective-permute-done.1.refs_2_.refs_5_ = bf16[128,640]{1,0:T(8,128)(2,1)S(1)} collective-permute-done((bf16[128,640]{1,0:T(8,128)(2,1)}, bf16[128,640]{1,0:T(8,128)(2,1)S(1)}, u32[]{:S(2)}, u32[]{:S(2)}) %collective-permute-start.1) | collective-permute-done | bytes 163872 | tf_op jit(solution)/shard_map/ppermute | solution.py:260
  12.9 0.0 collective-permute-start.2
  12.9 0.0 collective-permute-done.5.m2.refs_4_
  12.9 0.5 %collective-permute-start.6 = (bf16[128,640]{1,0:T(8,128)(2,1)S(1)}, bf16[128,640]{1,0:T(8,128)(2,1)S(1)}, u32[]{:S(2)}, u32[]{:S(2)}) collective-permute-start(bf16[128,640]{1,0:T(8,128)(2,1)S(1)} %collective-permute-done.5.m2.refs_4_), channel_id=1, source_target_pairs={{0,16},{16,0},{1,17},{17,1},{2,18},{18,2},{3,19},{19,3},{4,20},{20... | collective-permute-start | bytes 491528 | tf_op jit(solution)/shard_map/ppermute | solution.py:274
  13.4 0.0 copy-start
  13.4 1.2 %copy-done = bf16[128,3584]{1,0:T(8,128)(2,1)S(1)} copy-done((bf16[128,3584]{1,0:T(8,128)(2,1)S(1)}, bf16[128,3584]{1,0:T(8,128)(2,1)}, u32[]{:S(2)}) %copy-start) | copy-done | bytes 917528
  14.6 0.0 copy-start.1
  14.6 0.9 %copy-done.1 = bf16[1,128,640]{2,1,0:T(8,128)(2,1)S(1)} copy-done((bf16[1,128,640]{2,1,0:T(8,128)(2,1)S(1)}, bf16[1,128,640]{2,1,0:T(8,128)(2,1)}, u32[]{:S(2)}) %copy-start.1) | copy-done | bytes 163864
  15.5 0.0 copy-start.2
  15.5 0.7 %copy-done.2 = s32[8]{0:T(128)S(1)} copy-done((s32[8]{0:T(128)S(1)}, s32[8]{0:T(128)}, u32[]{:S(2)}) %copy-start.2) | copy-done | bytes 56
  16.2 0.9 %prepare.1 = (f32[128,128]{1,0:T(8,128)S(1)}, bf16[448,128]{1,0:T(8,128)(2,1)S(1)}, s32[8,8,128]{2,1,0:T(8,128)S(1)}, bf16[128,640]{1,0:T(8,128)(2,1)S(1)}) custom-call(s32[8]{0:T(128)S(1)} %copy-done.2, bf16[128,3584]{1,0:T(8,128)(2,1)S(1)} %copy-done, bf16[128,640]{1,0:T(8,128)(2,1)S(1)} %bitcast.9), custom_call_target="tpu_custom_call" | custom-call | flops 117440512 | tf_op jit(solution)/shard_map/prepare/pallas_call | solution.py:59
  17.1 0.0 collective-permute-done.refs_1_.refs_6_
  17.1 0.0 collective-permute-done.4.refs_5_.refs_7_
  17.1 0.0 collective-permute-done.2.refs_3_.refs_9_
  17.1 0.9 %early_gram.1 = (bf16[8,128,640]{2,1,0:T(8,128)(2,1)S(1)}, f32[8,8,128]{2,1,0:T(8,128)S(1)}) custom-call(bf16[128,640]{1,0:T(8,128)(2,1)S(1)} %get-tuple-element.10.refs_0_.refs_2_, bf16[128,640]{1,0:T(8,128)(2,1)S(1)} %collective-permute-done.refs_1_.refs_6_, bf16[128,640]{1,0:T(8,128)(2,1)S(1)} %collective-permute-done.1.refs_2_.refs_5_, ...), custom_call_target="tpu_custom_call" | custom-call | flops 503316480 | tf_op jit(solution)/shard_map/early_gram/pallas_call | solution.py:147
  18.0 0.0 collective-permute-done.6.o2.refs_8_
  18.0 0.8 %late_gram.1 = (f32[16,128]{1,0:T(8,128)S(1)}, bf16[8,128,640]{2,1,0:T(8,128)(2,1)S(1)}, f32[8,8,128]{2,1,0:T(8,128)S(1)}) custom-call(bf16[8,128,640]{2,1,0:T(8,128)(2,1)S(1)} %get-tuple-element.12.flat_in_ref, f32[8,8,128]{2,1,0:T(8,128)S(1)} %get-tuple-element.13.rows_in_ref, ...), custom_call_target="tpu_custom_call", output_to_operand_aliasing={{1}: (0, {}), {2}: (1, {})} | custom-call | flops 335544320 | tf_op jit(solution)/shard_map/late_gram/pallas_call | solution.py:156
  18.8 12.3 %all_to_all.11 = f32[16,1,128]{2,1,0:T(1,128)S(1)} all-to-all(f32[16,1,128]{2,1,0:T(1,128)S(1)} %bitcast.11), channel_id=1, replica_groups={{10,0,1,2,3,4,5,6,7,8,9,11,12,13,14,15},{26,16,17,18,19,20,21,22,23,24,..., dimensions={0} | all-to-all | bytes 16384 | tf_op jit(solution)/shard_map/all_to_all | solution.py:278
  31.1 1.7 %finish.1 = (f32[448,640]{1,0:T(8,128)}, f32[8]{0:T(128)}) custom-call(s32[8,8,128]{2,1,0:T(8,128)S(1)} %get-tuple-element.9.refs_0_, f32[16,128]{1,0:T(8,128)S(1)} %bitcast.10, bf16[128,640]{1,0:T(8,128)(2,1)S(1)} %get-tuple-element.10.refs_0_.refs_2_, bf16[128,640]{1,0:T(8,128)(2,1)S(1)} %collective-permute-done.3.refs_4_.refs_3_, ...), custom_call_target="tpu_custom_call" | custom-call | flops 73400320 | bytes 1146880 | tf_op jit(solution)/shard_map/finish/pallas_call | solution.py:231
Async XLA Ops:
  0.6 6.1 %collective-permute-start.3 = (bf16[128,640]{1,0:T(8,128)(2,1)}, bf16[128,640]{1,0:T(8,128)(2,1)S(1)}, u32[]{:S(2)}, u32[]{:S(2)}) collective-permute-start(bf16[128,640]{1,0:T(8,128)(2,1)} %bitcast.5), channel_id=1, source_target_pairs={{32,0},{48,16},{0,32},{16,48},{96,64},{112,80},{64,96},{80,112},{3... | collective-permute-start | bytes 491528 | tf_op jit(solution)/shard_map/ppermute | solution.py:260
  2.3 10.6 %collective-permute-start.1 = (bf16[128,640]{1,0:T(8,128)(2,1)}, bf16[128,640]{1,0:T(8,128)(2,1)S(1)}, u32[]{:S(2)}, u32[]{:S(2)}) collective-permute-start(bf16[128,640]{1,0:T(8,128)(2,1)} %bitcast.6), channel_id=1, source_target_pairs={{96,0},{112,16},{64,32},{80,48},{32,64},{48,80},{0,96},{16,112},{9... | collective-permute-start | bytes 491528 | tf_op jit(solution)/shard_map/ppermute | solution.py:260
  4.4 8.5 %collective-permute-start.5 = (bf16[128,640]{1,0:T(8,128)(2,1)}, bf16[128,640]{1,0:T(8,128)(2,1)S(1)}, u32[]{:S(2)}, u32[]{:S(2)}) collective-permute-start(bf16[128,640]{1,0:T(8,128)(2,1)} %bitcast.7), channel_id=1, source_target_pairs={{80,0},{64,16},{112,32},{96,48},{16,64},{0,80},{48,96},{32,112},{8... | collective-permute-start | bytes 491528 | tf_op jit(solution)/shard_map/ppermute | solution.py:260
  4.4 12.7 %collective-permute-start = (bf16[128,640]{1,0:T(8,128)(2,1)}, bf16[128,640]{1,0:T(8,128)(2,1)S(1)}, u32[]{:S(2)}, u32[]{:S(2)}) collective-permute-start(bf16[128,640]{1,0:T(8,128)(2,1)} %bitcast.8), channel_id=1, source_target_pairs={{0,16},{16,0},{1,17},{17,1},{2,18},{18,2},{3,19},{19,3},{4,20},{20... | collective-permute-start | bytes 491528 | tf_op jit(solution)/shard_map/ppermute | solution.py:274
  6.7 10.4 %collective-permute-start.4 = (bf16[128,640]{1,0:T(8,128)(2,1)S(1)}, bf16[128,640]{1,0:T(8,128)(2,1)S(1)}, u32[]{:S(2)}, u32[]{:S(2)}) collective-permute-start(bf16[128,640]{1,0:T(8,128)(2,1)S(1)} %collective-permute-done.3.refs_4_.refs_3_), channel_id=1, source_target_pairs={{0,16},{16,0},{1,17},{17,1},{2,18},{18,2},{3,19},{19,3},{4,20},{20... | collective-permute-start | bytes 491528 | tf_op jit(solution)/shard_map/ppermute | solution.py:274
  12.9 4.2 %collective-permute-start.2 = (bf16[128,640]{1,0:T(8,128)(2,1)S(1)}, bf16[128,640]{1,0:T(8,128)(2,1)S(1)}, u32[]{:S(2)}, u32[]{:S(2)}) collective-permute-start(bf16[128,640]{1,0:T(8,128)(2,1)S(1)} %collective-permute-done.1.refs_2_.refs_5_), channel_id=1, source_target_pairs={{0,16},{16,0},{1,17},{17,1},{2,18},{18,2},{3,19},{19,3},{4,20},{20... | collective-permute-start | bytes 491528 | tf_op jit(solution)/shard_map/ppermute | solution.py:274
  12.9 5.1 %collective-permute-start.6 = (bf16[128,640]{1,0:T(8,128)(2,1)S(1)}, bf16[128,640]{1,0:T(8,128)(2,1)S(1)}, u32[]{:S(2)}, u32[]{:S(2)}) collective-permute-start(bf16[128,640]{1,0:T(8,128)(2,1)S(1)} %collective-permute-done.5.m2.refs_4_), channel_id=1, source_target_pairs={{0,16},{16,0},{1,17},{17,1},{2,18},{18,2},{3,19},{19,3},{4,20},{20... | collective-permute-start | bytes 491528 | tf_op jit(solution)/shard_map/ppermute | solution.py:274
  13.4 1.2 %copy-start = (bf16[128,3584]{1,0:T(8,128)(2,1)S(1)}, bf16[128,3584]{1,0:T(8,128)(2,1)}, u32[]{:S(2)}) copy-start(bf16[128,3584]{1,0:T(8,128)(2,1)} %acts_hbm.1) | copy-start | bytes 2752516
  14.6 0.9 %copy-start.1 = (bf16[1,128,640]{2,1,0:T(8,128)(2,1)S(1)}, bf16[1,128,640]{2,1,0:T(8,128)(2,1)}, u32[]{:S(2)}) copy-start(bf16[1,128,640]{2,1,0:T(8,128)(2,1)} %param.4) | copy-start | bytes 491524
  15.5 0.7 %copy-start.2 = (s32[8]{0:T(128)S(1)}, s32[8]{0:T(128)}, u32[]{:S(2)}) copy-start(s32[8]{0:T(128)} %order_hbm.1) | copy-start | bytes 100
